TPU v7x, 32 devices: a whole 2x2x4 slice. The times are simulated.
32 devices in a mesh: gx: 4 (over y, x), gy: 2 (over core), gz: 4 (over z).
Axes of the slice: x: 2, y: 2, z: 4, core: 2. Of those that a mesh axis runs over, the one named last changes fastest.
Arguments:
- right_side: float32 [8, 32, 64, 512], P(None, 'gx', 'gy', 'gz'), may hold values from -12 to 12
- shift: float32 [32, 64, 512], P('gx', 'gy', 'gz'), may hold values from 0.02 to 2
Outputs:
- solution_block: float32 [8, 32, 64, 512], P(None, 'gx', 'gy', 'gz')
- residual_norms: float32 [8], replicated
All inputs are finite; a program needn't handle non-finite values.
Results may differ from a plain program's by a relative error of at most 0.0003.
Values sent between devices are 32-bit elements; how exact they have to be, the bound alone decides.
No kernel may reach another device: no remote copies, remote signals or barrier semaphores. Data moves between devices by JAX's collectives and lax.ppermute only.
A program may use at most 128 MiB of HBM per device.

v0:
```python
import jax
import jax.numpy as jnp
from jax import lax
from jax.sharding import PartitionSpec as P

ITERS = 2


def padded_2(block, sides, width):
    for axis, dim in sides:
        count = lax.axis_size(axis)
        forward = [(i, i + 1) for i in range(count - 1)]
        backward = [(target, source) for source, target in forward]
        low = lax.ppermute(
            lax.slice_in_dim(block, block.shape[dim] - width, None, axis=dim), axis, forward
        )
        high = lax.ppermute(lax.slice_in_dim(block, 0, width, axis=dim), axis, backward)
        block = jnp.concatenate([low, block, high], axis=dim)
    return block


def operate(fields, shift):
    padded = padded_2(fields, (("gx", 1), ("gy", 2), ("gz", 3)), 1)
    beside = padded[:, 2:, 1:-1, 1:-1] + padded[:, :-2, 1:-1, 1:-1]
    beside = beside + padded[:, 1:-1, 2:, 1:-1] + padded[:, 1:-1, :-2, 1:-1]
    beside = beside + padded[:, 1:-1, 1:-1, 2:] + padded[:, 1:-1, 1:-1, :-2]
    return (6.0 + shift)[None] * fields - beside


def lower_inverse(lower):
    count = lower.shape[0]
    return jax.scipy.linalg.solve_triangular(lower, jnp.eye(count, dtype=lower.dtype), lower=True)


def small_dot(left, right):
    return jnp.dot(left, right, precision=lax.Precision.HIGHEST)


def body(right_side, shift):
    width = right_side.shape[0]
    shape = right_side.shape
    rows = right_side.reshape(width, -1)
    gram = lax.psum(small_dot(rows, rows.T), ("gx", "gy", "gz"))
    lower = jnp.linalg.cholesky(gram)
    start_coeff = lower.T
    basis = [small_dot(lower_inverse(lower), rows)]
    hessen = jnp.zeros(((ITERS + 1) * width, ITERS * width), jnp.float32)
    for step in range(ITERS):
        image = operate(basis[step].reshape(shape), shift).reshape(width, -1)
        stacked = jnp.concatenate(basis, axis=0)
        products = lax.psum(
            small_dot(jnp.concatenate([stacked, image], axis=0), image.T), ("gx", "gy", "gz")
        )
        coeffs = products[:-width]
        gram = products[-width:] - small_dot(coeffs.T, coeffs)
        projected = image - small_dot(coeffs.T, stacked)
        lower = jnp.linalg.cholesky(gram)
        hessen = hessen.at[: (step + 1) * width, step * width : (step + 1) * width].set(coeffs)
        hessen = hessen.at[
            (step + 1) * width : (step + 2) * width, step * width : (step + 1) * width
        ].set(lower.T)
        if step + 1 < ITERS:
            basis.append(small_dot(lower_inverse(lower), projected))
    target = jnp.zeros(((ITERS + 1) * width, width), jnp.float32).at[:width].set(start_coeff)
    normal = small_dot(hessen.T, hessen)
    factor = jnp.linalg.cholesky(normal)
    coeff_y = jax.scipy.linalg.cho_solve((factor, True), small_dot(hessen.T, target))
    solution = small_dot(coeff_y.T, jnp.concatenate(basis, axis=0)).reshape(shape)
    leftover = target - small_dot(hessen, coeff_y)
    norms = jnp.sqrt(jnp.sum(leftover * leftover, axis=0))
    return (solution, norms)


def solution(mesh):
    in_specs = (P(None, "gx", "gy", "gz"), P("gx", "gy", "gz"))
    out_specs = (P(None, "gx", "gy", "gz"), P())
    return jax.shard_map(body, mesh=mesh, in_specs=in_specs, out_specs=out_specs, check_vma=False)
```

profile of v0, /device:TPU:0, one launch (start us, length us, event | category | flops | bytes accessed | tf_op | source)
XLA Modules:
  0.0 228.1 jit_solution(12695287434098205644)
XLA Ops:
  0.6 4.9 %convolution_bitcast_fusion = f32[8,8]{0,1:T(8,128)S(1)} fusion(f32[8,8,32,128]{3,2,1,0:T(8,128)} %param.15), kind=kOutput, calls=%fused_computation.19 | convolution fusion | flops 25165824 | bytes 1048832 | tf_op jit(solution)/shard_map/dot_general | solution.py:36
  5.5 42.0 %psum.21 = f32[8,8]{0,1:T(8,128)S(1)} all-reduce(f32[8,8]{0,1:T(8,128)S(1)} %convolution_bitcast_fusion), channel_id=1, replica_groups=mesh['gx'=4,'gy'=2,'gz'=4] {'gx','gy','gz'}, use_global_device_ids=true, to_apply=%region_0.0 | all-reduce | flops 64 | bytes 512 | tf_op jit(solution)/shard_map/psum | solution.py:43
  47.5 0.7 cholesky.94
  50.4 1.5 fusion.12
  51.9 1.3 collective-permute-start
  53.2 4.8 %collective-permute-start.1 = (f32[8,1,32,128]{3,0,2,1:T(8,128)S(1)}, f32[8,1,32,128]{3,0,2,1:T(8,128)S(1)}, u32[]{:S(2)}, u32[]{:S(2)}) collective-permute-start(f32[8,1,32,128]{3,0,2,1:T(8,128)S(1)} %get-tuple-element.84), channel_id=1, source_target_pairs={{0,8},{8,16},{16,24},{1,9},{9,17},{17,25},{2,10},{10,18},{18,26},{... | collective-permute-start | bytes 393224 | tf_op jit(solution)/shard_map/ppermute | solution.py:14
  58.1 1.0 collective-permute-done
  59.1 1.5 collective-permute-done.1
  60.6 1.3 collective-permute-start.2
  61.9 3.0 %collective-permute-start.3 = (f32[8,10,1,128]{3,0,2,1:T(8,128)S(1)}, f32[8,10,1,128]{3,0,2,1:T(8,128)S(1)}, u32[]{:S(2)}, u32[]{:S(2)}) collective-permute-start(f32[8,10,1,128]{3,0,2,1:T(8,128)S(1)} %get-tuple-element.80), channel_id=1, source_target_pairs={{0,4},{1,5},{2,6},{3,7},{8,12},{9,13},{10,14},{11,15},{16,20},{17,... | collective-permute-start | bytes 122888 | tf_op jit(solution)/shard_map/ppermute | solution.py:14
  64.9 0.8 collective-permute-done.3
  66.4 1.5 fusion.56
  67.9 2.0 copy.130
  70.0 1.3 collective-permute-start.4
  71.2 0.7 copy.132
  71.9 4.5 %collective-permute-start.5 = (f32[8,10,34,1]{2,0,3,1:T(8,128)S(1)}, f32[8,10,34,1]{2,0,3,1:T(8,128)S(1)}, u32[]{:S(2)}, u32[]{:S(2)}) collective-permute-start(f32[8,10,34,1]{2,0,3,1:T(8,128)S(1)} %copy.132), channel_id=1, source_target_pairs={{0,1},{1,2},{2,3},{4,5},{5,6},{6,7},{8,9},{9,10},{10,11},{12,13},{... | collective-permute-start | bytes 32648 | tf_op jit(solution)/shard_map/ppermute | solution.py:14
  77.1 0.7 copy.131
  78.1 1.8 copy.133
  79.9 3.0 %fusion.22 = f32[8,8,32,128]{3,0,2,1:T(8,128)S(1)} fusion(f32[8,10,34,1]{3,0,2,1:T(8,128)} %copy.133, f32[8,10,1,128]{3,0,2,1:T(8,128)S(1)} %collective-permute-done.2, f32[8,10,1,128]{3,0,2,1:T(8,128)} %copy-done.6, f32[8,1,32,128]{3,0,2,1:T(8,128)} %copy-done.3, f32[8,8,32,128]{3,0,2,1:T(8,128)S(1)} %bitcast.73, f32[8,1,32,128]{3,0,2,1:T(8,128)} %copy-done.4, ...), kind=kLoop, calls=%fused_computation.50 | loop fusion | flops 6553600 | bytes 2594048 | tf_op jit(solution)/shard_map/sub | solution.py:27
  82.9 2.6 %fusion.6 = f32[16,8]{0,1:T(8,128)S(1)} fusion(f32[8,32768]{1,0:T(8,128)S(1)} %bitcast.78, f32[8,32768]{1,0:T(8,128)S(1)} %fusion.12), kind=kOutput, calls=%fused_computation.9 | convolution fusion | flops 50855936 | bytes 2097664 | tf_op jit(solution)/shard_map/dot_general | solution.py:36
  85.5 43.2 %psum.22 = f32[16,8]{0,1:T(8,128)S(1)} all-reduce(f32[16,8]{0,1:T(8,128)S(1)} %fusion.6), channel_id=1, replica_groups=mesh['gx'=4,'gy'=2,'gz'=4] {'gx','gy','gz'}, use_global_device_ids=true, to_apply=%region_3.0 | all-reduce | flops 128 | bytes 1024 | tf_op jit(solution)/shard_map/psum | solution.py:51
  128.6 1.0 convolution_subtract_fusion
  129.8 0.7 cholesky.105
  132.7 1.0 fusion.60
  133.7 1.3 collective-permute-start.6
  135.0 4.8 %collective-permute-start.7 = (f32[8,1,32,128]{3,0,2,1:T(8,128)S(1)}, f32[8,1,32,128]{3,0,2,1:T(8,128)S(1)}, u32[]{:S(2)}, u32[]{:S(2)}) collective-permute-start(f32[8,1,32,128]{3,0,2,1:T(8,128)S(1)} %get-tuple-element.82), channel_id=1, source_target_pairs={{0,8},{8,16},{16,24},{1,9},{9,17},{17,25},{2,10},{10,18},{18,26},{... | collective-permute-start | bytes 393224 | tf_op jit(solution)/shard_map/ppermute | solution.py:14
  139.9 1.2 collective-permute-done.6
  141.1 1.3 collective-permute-done.7
  142.4 1.3 collective-permute-start.8
  143.7 3.0 %collective-permute-start.9 = (f32[8,10,1,128]{3,0,2,1:T(8,128)S(1)}, f32[8,10,1,128]{3,0,2,1:T(8,128)S(1)}, u32[]{:S(2)}, u32[]{:S(2)}) collective-permute-start(f32[8,10,1,128]{3,0,2,1:T(8,128)S(1)} %get-tuple-element.78), channel_id=1, source_target_pairs={{0,4},{1,5},{2,6},{3,7},{8,12},{9,13},{10,14},{11,15},{16,20},{17,... | collective-permute-start | bytes 122888 | tf_op jit(solution)/shard_map/ppermute | solution.py:14
  146.7 0.8 collective-permute-done.9
  148.3 1.5 fusion.55
  149.8 2.6 %copy.137 = f32[8,10,34,1]{2,0,3,1:T(8,128)} copy(f32[8,10,34,1]{3,0,2,1:T(8,128)} %get-tuple-element.74) | data formatting | bytes 21760 | tf_op jit(solution)/shard_map/slice | solution.py:17
  152.4 1.3 collective-permute-start.10
  153.7 1.3 copy.139
  155.0 5.2 %collective-permute-start.11 = (f32[8,10,34,1]{2,0,3,1:T(8,128)}, f32[8,10,34,1]{2,0,3,1:T(8,128)}, u32[]{:S(2)}, u32[]{:S(2)}) collective-permute-start(f32[8,10,34,1]{2,0,3,1:T(8,128)} %copy.139), channel_id=1, source_target_pairs={{0,1},{1,2},{2,3},{4,5},{5,6},{6,7},{8,9},{9,10},{10,11},{12,13},{... | collective-permute-start | bytes 32648 | tf_op jit(solution)/shard_map/ppermute | solution.py:14
  161.8 1.5 copy.138
  163.3 2.6 %copy.140 = f32[8,10,34,1]{3,0,2,1:T(8,128)} copy(f32[8,10,34,1]{2,0,3,1:T(8,128)} %collective-permute-done.11) | data formatting | bytes 21760 | tf_op jit(solution)/shard_map/ppermute | solution.py:14
  165.8 3.0 %fusion.16 = f32[8,8,32,128]{3,0,2,1:T(8,128)S(1)} fusion(f32[8,10,34,1]{3,0,2,1:T(8,128)} %copy.140, f32[8,10,1,128]{3,0,2,1:T(8,128)S(1)} %collective-permute-done.8, f32[8,10,1,128]{3,0,2,1:T(8,128)} %copy-done.5, f32[8,1,32,128]{3,0,2,1:T(8,128)} %copy-done.1, f32[8,8,32,128]{3,0,2,1:T(8,128)S(1)} %bitcast.77, f32[8,1,32,128]{3,0,2,1:T(8,128)} %copy-done.2, ...), kind=kLoop, calls=%fused_computation.26 | loop fusion | flops 6553600 | bytes 2594048 | tf_op jit(solution)/shard_map/sub | solution.py:27
  168.9 3.0 %fusion = f32[24,8]{0,1:T(8,128)S(1)} fusion(f32[8,32768]{1,0:T(8,128)S(1)} %bitcast.82, f32[8,32768]{1,0:T(8,128)S(1)} %fusion.60, f32[8,32768]{1,0:T(8,128)S(1)} %fusion.12), kind=kOutput, calls=%fused_computation.1 | convolution fusion | flops 77070336 | bytes 3146496 | tf_op jit(solution)/shard_map/dot_general | solution.py:36
  171.9 42.0 %psum.23 = f32[24,8]{0,1:T(8,128)S(1)} all-reduce(f32[24,8]{0,1:T(8,128)S(1)} %fusion), channel_id=1, replica_groups=mesh['gx'=4,'gy'=2,'gz'=4] {'gx','gy','gz'}, use_global_device_ids=true, to_apply=%region_5.0 | all-reduce | flops 192 | bytes 1536 | tf_op jit(solution)/shard_map/psum | solution.py:51
  214.0 0.7 cholesky.116
  216.1 2.0 dynamic-slice_select_fusion
  218.1 1.7 scatter.20
  220.6 1.5 cholesky.41
  223.4 1.2 custom-call.15
  225.3 1.1 fusion.7
  227.0 1.2 copy.144
  (67 shorter events, 13.4 us)
Async XLA Ops:
  0.6 49.8 %copy-start = (f32[8,8,32,128]{3,2,1,0:T(8,128)S(1)}, f32[8,8,32,128]{3,2,1,0:T(8,128)}, u32[]{:S(2)}) copy-start(f32[8,8,32,128]{3,2,1,0:T(8,128)} %param.15) | copy-start | bytes 3145732
  51.9 7.1 %collective-permute-start = (f32[8,1,32,128]{3,0,2,1:T(8,128)S(1)}, f32[8,1,32,128]{3,0,2,1:T(8,128)S(1)}, u32[]{:S(2)}, u32[]{:S(2)}) collective-permute-start(f32[8,1,32,128]{3,0,2,1:T(8,128)S(1)} %get-tuple-element.85), channel_id=1, source_target_pairs={{8,0},{16,8},{24,16},{9,1},{17,9},{25,17},{10,2},{18,10},{26,18},{... | collective-permute-start | bytes 393224 | tf_op jit(solution)/shard_map/ppermute | solution.py:17
  53.2 7.3 %collective-permute-start.1 = (f32[8,1,32,128]{3,0,2,1:T(8,128)S(1)}, f32[8,1,32,128]{3,0,2,1:T(8,128)S(1)}, u32[]{:S(2)}, u32[]{:S(2)}) collective-permute-start(f32[8,1,32,128]{3,0,2,1:T(8,128)S(1)} %get-tuple-element.84), channel_id=1, source_target_pairs={{0,8},{8,16},{16,24},{1,9},{9,17},{17,25},{2,10},{10,18},{18,26},{... | collective-permute-start | bytes 393224 | tf_op jit(solution)/shard_map/ppermute | solution.py:14
  59.1 6.8 %copy-start.3 = (f32[8,1,32,128]{3,0,2,1:T(8,128)}, f32[8,1,32,128]{3,0,2,1:T(8,128)S(1)}, u32[]{:S(2)}) copy-start(f32[8,1,32,128]{3,0,2,1:T(8,128)S(1)} %collective-permute-done) | copy-start | bytes 393220
  60.6 5.3 %copy-start.4 = (f32[8,1,32,128]{3,0,2,1:T(8,128)}, f32[8,1,32,128]{3,0,2,1:T(8,128)S(1)}, u32[]{:S(2)}) copy-start(f32[8,1,32,128]{3,0,2,1:T(8,128)S(1)} %collective-permute-done.1) | copy-start | bytes 393220
  60.6 4.3 %collective-permute-start.2 = (f32[8,10,1,128]{3,0,2,1:T(8,128)S(1)}, f32[8,10,1,128]{3,0,2,1:T(8,128)S(1)}, u32[]{:S(2)}, u32[]{:S(2)}) collective-permute-start(f32[8,10,1,128]{3,0,2,1:T(8,128)S(1)} %get-tuple-element.81), channel_id=1, source_target_pairs={{4,0},{5,1},{6,2},{7,3},{12,8},{13,9},{14,10},{15,11},{20,16},{21,... | collective-permute-start | bytes 122888 | tf_op jit(solution)/shard_map/ppermute | solution.py:17
  61.9 3.9 %collective-permute-start.3 = (f32[8,10,1,128]{3,0,2,1:T(8,128)S(1)}, f32[8,10,1,128]{3,0,2,1:T(8,128)S(1)}, u32[]{:S(2)}, u32[]{:S(2)}) collective-permute-start(f32[8,10,1,128]{3,0,2,1:T(8,128)S(1)} %get-tuple-element.80), channel_id=1, source_target_pairs={{0,4},{1,5},{2,6},{3,7},{8,12},{9,13},{10,14},{11,15},{16,20},{17,... | collective-permute-start | bytes 122888 | tf_op jit(solution)/shard_map/ppermute | solution.py:14
  65.8 0.6 copy-start.6
  67.9 8.5 %copy-start.7 = (f32[8,32,128]{2,1,0:T(8,128)S(1)}, f32[8,32,128]{2,1,0:T(8,128)}, u32[]{:S(2)}) copy-start(f32[8,32,128]{2,1,0:T(8,128)} %param.16) | copy-start | bytes 393220
  70.0 7.2 %collective-permute-start.4 = (f32[8,10,34,1]{2,0,3,1:T(8,128)S(1)}, f32[8,10,34,1]{2,0,3,1:T(8,128)S(1)}, u32[]{:S(2)}, u32[]{:S(2)}) collective-permute-start(f32[8,10,34,1]{2,0,3,1:T(8,128)S(1)} %copy.130), channel_id=1, source_target_pairs={{1,0},{2,1},{3,2},{5,4},{6,5},{7,6},{9,8},{10,9},{11,10},{13,12},{... | collective-permute-start | bytes 32648 | tf_op jit(solution)/shard_map/ppermute | solution.py:17
  71.9 6.2 %collective-permute-start.5 = (f32[8,10,34,1]{2,0,3,1:T(8,128)S(1)}, f32[8,10,34,1]{2,0,3,1:T(8,128)S(1)}, u32[]{:S(2)}, u32[]{:S(2)}) collective-permute-start(f32[8,10,34,1]{2,0,3,1:T(8,128)S(1)} %copy.132), channel_id=1, source_target_pairs={{0,1},{1,2},{2,3},{4,5},{5,6},{6,7},{8,9},{9,10},{10,11},{12,13},{... | collective-permute-start | bytes 32648 | tf_op jit(solution)/shard_map/ppermute | solution.py:14
  133.7 7.3 %collective-permute-start.6 = (f32[8,1,32,128]{3,0,2,1:T(8,128)S(1)}, f32[8,1,32,128]{3,0,2,1:T(8,128)S(1)}, u32[]{:S(2)}, u32[]{:S(2)}) collective-permute-start(f32[8,1,32,128]{3,0,2,1:T(8,128)S(1)} %get-tuple-element.83), channel_id=1, source_target_pairs={{8,0},{16,8},{24,16},{9,1},{17,9},{25,17},{10,2},{18,10},{26,18},{... | collective-permute-start | bytes 393224 | tf_op jit(solution)/shard_map/ppermute | solution.py:17
  135.0 7.3 %collective-permute-start.7 = (f32[8,1,32,128]{3,0,2,1:T(8,128)S(1)}, f32[8,1,32,128]{3,0,2,1:T(8,128)S(1)}, u32[]{:S(2)}, u32[]{:S(2)}) collective-permute-start(f32[8,1,32,128]{3,0,2,1:T(8,128)S(1)} %get-tuple-element.82), channel_id=1, source_target_pairs={{0,8},{8,16},{16,24},{1,9},{9,17},{17,25},{2,10},{10,18},{18,26},{... | collective-permute-start | bytes 393224 | tf_op jit(solution)/shard_map/ppermute | solution.py:14
  141.1 6.5 %copy-start.1 = (f32[8,1,32,128]{3,0,2,1:T(8,128)}, f32[8,1,32,128]{3,0,2,1:T(8,128)S(1)}, u32[]{:S(2)}) copy-start(f32[8,1,32,128]{3,0,2,1:T(8,128)S(1)} %collective-permute-done.6) | copy-start | bytes 393220
  142.4 5.2 %copy-start.2 = (f32[8,1,32,128]{3,0,2,1:T(8,128)}, f32[8,1,32,128]{3,0,2,1:T(8,128)S(1)}, u32[]{:S(2)}) copy-start(f32[8,1,32,128]{3,0,2,1:T(8,128)S(1)} %collective-permute-done.7) | copy-start | bytes 393220
  142.4 4.4 %collective-permute-start.8 = (f32[8,10,1,128]{3,0,2,1:T(8,128)S(1)}, f32[8,10,1,128]{3,0,2,1:T(8,128)S(1)}, u32[]{:S(2)}, u32[]{:S(2)}) collective-permute-start(f32[8,10,1,128]{3,0,2,1:T(8,128)S(1)} %get-tuple-element.79), channel_id=1, source_target_pairs={{4,0},{5,1},{6,2},{7,3},{12,8},{13,9},{14,10},{15,11},{20,16},{21,... | collective-permute-start | bytes 122888 | tf_op jit(solution)/shard_map/ppermute | solution.py:17
  143.7 3.9 %collective-permute-start.9 = (f32[8,10,1,128]{3,0,2,1:T(8,128)S(1)}, f32[8,10,1,128]{3,0,2,1:T(8,128)S(1)}, u32[]{:S(2)}, u32[]{:S(2)}) collective-permute-start(f32[8,10,1,128]{3,0,2,1:T(8,128)S(1)} %get-tuple-element.78), channel_id=1, source_target_pairs={{0,4},{1,5},{2,6},{3,7},{8,12},{9,13},{10,14},{11,15},{16,20},{17,... | collective-permute-start | bytes 122888 | tf_op jit(solution)/shard_map/ppermute | solution.py:14
  147.6 0.6 copy-start.5
  152.4 9.4 %collective-permute-start.10 = (f32[8,10,34,1]{2,0,3,1:T(8,128)}, f32[8,10,34,1]{2,0,3,1:T(8,128)}, u32[]{:S(2)}, u32[]{:S(2)}) collective-permute-start(f32[8,10,34,1]{2,0,3,1:T(8,128)} %copy.137), channel_id=1, source_target_pairs={{1,0},{2,1},{3,2},{5,4},{6,5},{7,6},{9,8},{10,9},{11,10},{13,12},{... | collective-permute-start | bytes 32648 | tf_op jit(solution)/shard_map/ppermute | solution.py:17
  155.0 8.3 %collective-permute-start.11 = (f32[8,10,34,1]{2,0,3,1:T(8,128)}, f32[8,10,34,1]{2,0,3,1:T(8,128)}, u32[]{:S(2)}, u32[]{:S(2)}) collective-permute-start(f32[8,10,34,1]{2,0,3,1:T(8,128)} %copy.139), channel_id=1, source_target_pairs={{0,1},{1,2},{2,3},{4,5},{5,6},{6,7},{8,9},{9,10},{10,11},{12,13},{... | collective-permute-start | bytes 32648 | tf_op jit(solution)/shard_map/ppermute | solution.py:14
where the time goes:
time: 229 us; the launch traced here: 228 us
  blocking collectives  127 us (55%)
  starting transfers between devices  33.1 us (14%)
  local copies, waits for them, and re-layouts  22.6 us (10%)
  other arithmetic  21 us (9%)
  matrix products  16.4 us (7%)
  waiting for transfers between devices  6.95 us (3%)
    psum x2, blocking collectives, body(): lax.psum(small_dot(jnp.concatenate([stacked, image], axis=0), image.T), (...  85.1 us
    psum x1, blocking collectives, body(): gram = lax.psum(small_dot(rows, rows.T), ('gx', 'gy', 'gz'))  42 us
    ppermute x6, starting transfers between devices, padded_2(): lax.ppermute(lax.slice_in_dim(block, block.shape[dim] - width, None, axis...  25.4 us
    dot_general x12, matrix products, small_dot(): return jnp.dot(left, right, precision=lax.Precision.HIGHEST)  15.7 us
    ppermute x6, starting transfers between devices, padded_2(): lax.ppermute(lax.slice_in_dim(block, 0, width, axis=dim), axis, backward)  7.73 us
    slice x4, local copies, waits for them, and re-layouts, padded_2(): lax.slice_in_dim(block, 0, width, axis=dim)  7.72 us
    sub x2, other arithmetic, operate(): return (6.0 + shift)[None] * fields - beside  6.01 us
    ppermute x6, waiting for transfers between devices, padded_2(): lax.ppermute(lax.slice_in_dim(block, block.shape[dim] - width, None, axis...  4.75 us
  transfers between devices with their start and end apart: 12, of which 7 were waited for; matrix products, arithmetic and copies ran while one was open for 3% of the time, Pallas kernels for 0%

commit v1 on v0

--- a/solution.py
+++ b/solution.py
@@ -40,7 +40,7 @@
     width = right_side.shape[0]
     shape = right_side.shape
     rows = right_side.reshape(width, -1)
-    gram = lax.psum(small_dot(rows, rows.T), ("gx", "gy", "gz"))
+    gram = lax.psum(lax.psum(small_dot(rows, rows.T), "gx"), ("gy", "gz"))
     lower = jnp.linalg.cholesky(gram)
     start_coeff = lower.T
     basis = [small_dot(lower_inverse(lower), rows)]

time: 229 us -> 211 us (0.921)
  blocking collectives: 127 us -> 109 us
    psum x1 -> x2, blocking collectives: 42 us -> 26.8 us  [body(): gram = lax.psum(lax.psum(small_dot(rows, rows.T), 'gx'), ('gy', 'gz'))]
    psum x2, blocking collectives: 85.1 us -> 82.6 us  [body(): lax.psum(small_dot(jnp.concatenate([stacked, image], axis=0), image.T), (...]
where the time goes in v1:
time: 211 us; the launch traced here: 210 us
  blocking collectives  109 us (52%)
  starting transfers between devices  32.9 us (16%)
  local copies, waits for them, and re-layouts  22.1 us (10%)
  other arithmetic  21 us (10%)
  matrix products  16.4 us (8%)
  waiting for transfers between devices  7.56 us (4%)
    psum x2, blocking collectives, body(): lax.psum(small_dot(jnp.concatenate([stacked, image], axis=0), image.T), (...  82.6 us
    psum x2, blocking collectives, body(): gram = lax.psum(lax.psum(small_dot(rows, rows.T), 'gx'), ('gy', 'gz'))  26.8 us
    ppermute x6, starting transfers between devices, padded_2(): lax.ppermute(lax.slice_in_dim(block, block.shape[dim] - width, None, axis...  25.1 us
    dot_general x12, matrix products, small_dot(): return jnp.dot(left, right, precision=lax.Precision.HIGHEST)  15.7 us
    ppermute x6, starting transfers between devices, padded_2(): lax.ppermute(lax.slice_in_dim(block, 0, width, axis=dim), axis, backward)  7.73 us
    slice x4, local copies, waits for them, and re-layouts, padded_2(): lax.slice_in_dim(block, 0, width, axis=dim)  7.72 us
    sub x2, other arithmetic, operate(): return (6.0 + shift)[None] * fields - beside  6.01 us
    ppermute x6, waiting for transfers between devices, padded_2(): lax.ppermute(lax.slice_in_dim(block, block.shape[dim] - width, None, axis...  4.91 us
  transfers between devices with their start and end apart: 12, of which 7 were waited for; matrix products, arithmetic and copies ran while one was open for 3% of the time, Pallas kernels for 0%

profile of v1, /device:TPU:0, one launch (start us, length us, event | category | flops | bytes accessed | tf_op | source)
XLA Modules:
  0.0 210.3 jit_solution(2657746348880306665)
XLA Ops:
  0.6 4.9 %convolution_bitcast_fusion = f32[8,8]{0,1:T(8,128)S(1)} fusion(f32[8,8,32,128]{3,2,1,0:T(8,128)} %param.15), kind=kOutput, calls=%fused_computation.19 | convolution fusion | flops 25165824 | bytes 1048832 | tf_op jit(solution)/shard_map/dot_general | solution.py:36
  5.5 11.4 %psum.28 = f32[8,8]{0,1:T(8,128)S(1)} all-reduce(f32[8,8]{0,1:T(8,128)S(1)} %convolution_bitcast_fusion), channel_id=1, replica_groups=mesh['gx'=4,'gy'=2,'gz'=4] {'gx'}, use_global_device_ids=true, to_apply=%region_0.0 | all-reduce | flops 64 | bytes 512 | tf_op jit(solution)/shard_map/psum | solution.py:43
  16.9 15.4 %psum.29 = f32[8,8]{0,1:T(8,128)S(1)} all-reduce(f32[8,8]{0,1:T(8,128)S(1)} %psum.28), channel_id=1, replica_groups=mesh['gx'=4,'gy'=2,'gz'=4] {'gy','gz'}, use_global_device_ids=true, to_apply=%region_1.0 | all-reduce | flops 64 | bytes 512 | tf_op jit(solution)/shard_map/psum | solution.py:43
  32.4 0.7 cholesky.94
  35.2 1.5 fusion.12
  36.8 1.3 collective-permute-start
  38.1 4.6 %collective-permute-start.1 = (f32[8,1,32,128]{3,0,2,1:T(8,128)S(1)}, f32[8,1,32,128]{3,0,2,1:T(8,128)S(1)}, u32[]{:S(2)}, u32[]{:S(2)}) collective-permute-start(f32[8,1,32,128]{3,0,2,1:T(8,128)S(1)} %get-tuple-element.84), channel_id=1, source_target_pairs={{0,8},{8,16},{16,24},{1,9},{9,17},{17,25},{2,10},{10,18},{18,26},{... | collective-permute-start | bytes 393224 | tf_op jit(solution)/shard_map/ppermute | solution.py:14
  42.6 1.4 collective-permute-done
  44.0 1.7 collective-permute-done.1
  45.7 1.3 collective-permute-start.2
  47.0 3.0 %collective-permute-start.3 = (f32[8,10,1,128]{3,0,2,1:T(8,128)S(1)}, f32[8,10,1,128]{3,0,2,1:T(8,128)S(1)}, u32[]{:S(2)}, u32[]{:S(2)}) collective-permute-start(f32[8,10,1,128]{3,0,2,1:T(8,128)S(1)} %get-tuple-element.80), channel_id=1, source_target_pairs={{0,4},{1,5},{2,6},{3,7},{8,12},{9,13},{10,14},{11,15},{16,20},{17,... | collective-permute-start | bytes 122888 | tf_op jit(solution)/shard_map/ppermute | solution.py:14
  50.1 0.8 collective-permute-done.3
  51.1 1.5 fusion.56
  52.6 2.0 copy.130
  54.6 1.3 collective-permute-start.4
  56.6 4.5 %collective-permute-start.5 = (f32[8,10,34,1]{2,0,3,1:T(8,128)S(1)}, f32[8,10,34,1]{2,0,3,1:T(8,128)S(1)}, u32[]{:S(2)}, u32[]{:S(2)}) collective-permute-start(f32[8,10,34,1]{2,0,3,1:T(8,128)S(1)} %copy.132), channel_id=1, source_target_pairs={{0,1},{1,2},{2,3},{4,5},{5,6},{6,7},{8,9},{9,10},{10,11},{12,13},{... | collective-permute-start | bytes 32648 | tf_op jit(solution)/shard_map/ppermute | solution.py:14
  61.8 0.7 copy.131
  62.8 1.8 copy.133
  64.6 3.0 %fusion.22 = f32[8,8,32,128]{3,0,2,1:T(8,128)S(1)} fusion(f32[8,10,34,1]{3,0,2,1:T(8,128)} %copy.133, f32[8,10,1,128]{3,0,2,1:T(8,128)S(1)} %collective-permute-done.2, f32[8,10,1,128]{3,0,2,1:T(8,128)} %copy-done.6, f32[8,1,32,128]{3,0,2,1:T(8,128)} %copy-done.3, f32[8,8,32,128]{3,0,2,1:T(8,128)S(1)} %bitcast.73, f32[8,1,32,128]{3,0,2,1:T(8,128)} %copy-done.4, ...), kind=kLoop, calls=%fused_computation.50 | loop fusion | flops 6553600 | bytes 2594048 | tf_op jit(solution)/shard_map/sub | solution.py:27
  67.6 2.6 %fusion.6 = f32[16,8]{0,1:T(8,128)S(1)} fusion(f32[8,32768]{1,0:T(8,128)S(1)} %bitcast.78, f32[8,32768]{1,0:T(8,128)S(1)} %fusion.12), kind=kOutput, calls=%fused_computation.9 | convolution fusion | flops 50855936 | bytes 2097664 | tf_op jit(solution)/shard_map/dot_general | solution.py:36
  70.1 41.3 %psum.30 = f32[16,8]{0,1:T(8,128)S(1)} all-reduce(f32[16,8]{0,1:T(8,128)S(1)} %fusion.6), channel_id=1, replica_groups=mesh['gx'=4,'gy'=2,'gz'=4] {'gx','gy','gz'}, use_global_device_ids=true, to_apply=%region_4.0 | all-reduce | flops 128 | bytes 1024 | tf_op jit(solution)/shard_map/psum | solution.py:51
  111.5 1.0 convolution_subtract_fusion
  112.6 0.7 cholesky.105
  115.5 1.0 fusion.60
  116.6 1.3 collective-permute-start.6
  117.9 4.8 %collective-permute-start.7 = (f32[8,1,32,128]{3,0,2,1:T(8,128)S(1)}, f32[8,1,32,128]{3,0,2,1:T(8,128)S(1)}, u32[]{:S(2)}, u32[]{:S(2)}) collective-permute-start(f32[8,1,32,128]{3,0,2,1:T(8,128)S(1)} %get-tuple-element.82), channel_id=1, source_target_pairs={{0,8},{8,16},{16,24},{1,9},{9,17},{17,25},{2,10},{10,18},{18,26},{... | collective-permute-start | bytes 393224 | tf_op jit(solution)/shard_map/ppermute | solution.py:14
  122.7 1.3 collective-permute-done.6
  124.0 1.2 collective-permute-done.7
  125.2 1.3 collective-permute-start.8
  126.5 3.0 %collective-permute-start.9 = (f32[8,10,1,128]{3,0,2,1:T(8,128)S(1)}, f32[8,10,1,128]{3,0,2,1:T(8,128)S(1)}, u32[]{:S(2)}, u32[]{:S(2)}) collective-permute-start(f32[8,10,1,128]{3,0,2,1:T(8,128)S(1)} %get-tuple-element.78), channel_id=1, source_target_pairs={{0,4},{1,5},{2,6},{3,7},{8,12},{9,13},{10,14},{11,15},{16,20},{17,... | collective-permute-start | bytes 122888 | tf_op jit(solution)/shard_map/ppermute | solution.py:14
  129.6 0.8 collective-permute-done.9
  131.1 1.5 fusion.55
  132.6 2.6 %copy.137 = f32[8,10,34,1]{2,0,3,1:T(8,128)} copy(f32[8,10,34,1]{3,0,2,1:T(8,128)} %get-tuple-element.74) | data formatting | bytes 21760 | tf_op jit(solution)/shard_map/slice | solution.py:17
  135.3 1.3 collective-permute-start.10
  136.5 1.3 copy.139
  137.8 5.2 %collective-permute-start.11 = (f32[8,10,34,1]{2,0,3,1:T(8,128)}, f32[8,10,34,1]{2,0,3,1:T(8,128)}, u32[]{:S(2)}, u32[]{:S(2)}) collective-permute-start(f32[8,10,34,1]{2,0,3,1:T(8,128)} %copy.139), channel_id=1, source_target_pairs={{0,1},{1,2},{2,3},{4,5},{5,6},{6,7},{8,9},{9,10},{10,11},{12,13},{... | collective-permute-start | bytes 32648 | tf_op jit(solution)/shard_map/ppermute | solution.py:14
  144.7 1.5 copy.138
  146.1 2.6 %copy.140 = f32[8,10,34,1]{3,0,2,1:T(8,128)} copy(f32[8,10,34,1]{2,0,3,1:T(8,128)} %collective-permute-done.11) | data formatting | bytes 21760 | tf_op jit(solution)/shard_map/ppermute | solution.py:14
  148.7 3.0 %fusion.16 = f32[8,8,32,128]{3,0,2,1:T(8,128)S(1)} fusion(f32[8,10,34,1]{3,0,2,1:T(8,128)} %copy.140, f32[8,10,1,128]{3,0,2,1:T(8,128)S(1)} %collective-permute-done.8, f32[8,10,1,128]{3,0,2,1:T(8,128)} %copy-done.5, f32[8,1,32,128]{3,0,2,1:T(8,128)} %copy-done.1, f32[8,8,32,128]{3,0,2,1:T(8,128)S(1)} %bitcast.77, f32[8,1,32,128]{3,0,2,1:T(8,128)} %copy-done.2, ...), kind=kLoop, calls=%fused_computation.26 | loop fusion | flops 6553600 | bytes 2594048 | tf_op jit(solution)/shard_map/sub | solution.py:27
  151.7 3.0 %fusion = f32[24,8]{0,1:T(8,128)S(1)} fusion(f32[8,32768]{1,0:T(8,128)S(1)} %bitcast.82, f32[8,32768]{1,0:T(8,128)S(1)} %fusion.60, f32[8,32768]{1,0:T(8,128)S(1)} %fusion.12), kind=kOutput, calls=%fused_computation.1 | convolution fusion | flops 77070336 | bytes 3146496 | tf_op jit(solution)/shard_map/dot_general | solution.py:36
  154.7 41.3 %psum.31 = f32[24,8]{0,1:T(8,128)S(1)} all-reduce(f32[24,8]{0,1:T(8,128)S(1)} %fusion), channel_id=1, replica_groups=mesh['gx'=4,'gy'=2,'gz'=4] {'gx','gy','gz'}, use_global_device_ids=true, to_apply=%region_6.0 | all-reduce | flops 192 | bytes 1536 | tf_op jit(solution)/shard_map/psum | solution.py:51
  196.2 0.7 cholesky.116
  198.3 2.0 dynamic-slice_select_fusion
  200.3 1.7 scatter.20
  202.8 1.5 cholesky.41
  205.6 1.2 custom-call.15
  207.5 1.1 fusion.7
  209.1 1.2 copy.144
  (68 shorter events, 13.5 us)
Async XLA Ops:
  0.6 34.6 %copy-start = (f32[8,8,32,128]{3,2,1,0:T(8,128)S(1)}, f32[8,8,32,128]{3,2,1,0:T(8,128)}, u32[]{:S(2)}) copy-start(f32[8,8,32,128]{3,2,1,0:T(8,128)} %param.15) | copy-start | bytes 3145732
  36.8 7.2 %collective-permute-start = (f32[8,1,32,128]{3,0,2,1:T(8,128)S(1)}, f32[8,1,32,128]{3,0,2,1:T(8,128)S(1)}, u32[]{:S(2)}, u32[]{:S(2)}) collective-permute-start(f32[8,1,32,128]{3,0,2,1:T(8,128)S(1)} %get-tuple-element.85), channel_id=1, source_target_pairs={{8,0},{16,8},{24,16},{9,1},{17,9},{25,17},{10,2},{18,10},{26,18},{... | collective-permute-start | bytes 393224 | tf_op jit(solution)/shard_map/ppermute | solution.py:17
  38.1 7.7 %collective-permute-start.1 = (f32[8,1,32,128]{3,0,2,1:T(8,128)S(1)}, f32[8,1,32,128]{3,0,2,1:T(8,128)S(1)}, u32[]{:S(2)}, u32[]{:S(2)}) collective-permute-start(f32[8,1,32,128]{3,0,2,1:T(8,128)S(1)} %get-tuple-element.84), channel_id=1, source_target_pairs={{0,8},{8,16},{16,24},{1,9},{9,17},{17,25},{2,10},{10,18},{18,26},{... | collective-permute-start | bytes 393224 | tf_op jit(solution)/shard_map/ppermute | solution.py:14
  44.0 7.0 %copy-start.3 = (f32[8,1,32,128]{3,0,2,1:T(8,128)}, f32[8,1,32,128]{3,0,2,1:T(8,128)S(1)}, u32[]{:S(2)}) copy-start(f32[8,1,32,128]{3,0,2,1:T(8,128)S(1)} %collective-permute-done) | copy-start | bytes 393220
  45.7 5.3 %copy-start.4 = (f32[8,1,32,128]{3,0,2,1:T(8,128)}, f32[8,1,32,128]{3,0,2,1:T(8,128)S(1)}, u32[]{:S(2)}) copy-start(f32[8,1,32,128]{3,0,2,1:T(8,128)S(1)} %collective-permute-done.1) | copy-start | bytes 393220
  45.7 4.3 %collective-permute-start.2 = (f32[8,10,1,128]{3,0,2,1:T(8,128)S(1)}, f32[8,10,1,128]{3,0,2,1:T(8,128)S(1)}, u32[]{:S(2)}, u32[]{:S(2)}) collective-permute-start(f32[8,10,1,128]{3,0,2,1:T(8,128)S(1)} %get-tuple-element.81), channel_id=1, source_target_pairs={{4,0},{5,1},{6,2},{7,3},{12,8},{13,9},{14,10},{15,11},{20,16},{21,... | collective-permute-start | bytes 122888 | tf_op jit(solution)/shard_map/ppermute | solution.py:17
  47.0 3.9 %collective-permute-start.3 = (f32[8,10,1,128]{3,0,2,1:T(8,128)S(1)}, f32[8,10,1,128]{3,0,2,1:T(8,128)S(1)}, u32[]{:S(2)}, u32[]{:S(2)}) collective-permute-start(f32[8,10,1,128]{3,0,2,1:T(8,128)S(1)} %get-tuple-element.80), channel_id=1, source_target_pairs={{0,4},{1,5},{2,6},{3,7},{8,12},{9,13},{10,14},{11,15},{16,20},{17,... | collective-permute-start | bytes 122888 | tf_op jit(solution)/shard_map/ppermute | solution.py:14
  50.9 1.7 copy-start.6
  52.6 8.5 %copy-start.7 = (f32[8,32,128]{2,1,0:T(8,128)S(1)}, f32[8,32,128]{2,1,0:T(8,128)}, u32[]{:S(2)}) copy-start(f32[8,32,128]{2,1,0:T(8,128)} %param.16) | copy-start | bytes 393220
  54.6 7.2 %collective-permute-start.4 = (f32[8,10,34,1]{2,0,3,1:T(8,128)S(1)}, f32[8,10,34,1]{2,0,3,1:T(8,128)S(1)}, u32[]{:S(2)}, u32[]{:S(2)}) collective-permute-start(f32[8,10,34,1]{2,0,3,1:T(8,128)S(1)} %copy.130), channel_id=1, source_target_pairs={{1,0},{2,1},{3,2},{5,4},{6,5},{7,6},{9,8},{10,9},{11,10},{13,12},{... | collective-permute-start | bytes 32648 | tf_op jit(solution)/shard_map/ppermute | solution.py:17
  56.6 6.2 %collective-permute-start.5 = (f32[8,10,34,1]{2,0,3,1:T(8,128)S(1)}, f32[8,10,34,1]{2,0,3,1:T(8,128)S(1)}, u32[]{:S(2)}, u32[]{:S(2)}) collective-permute-start(f32[8,10,34,1]{2,0,3,1:T(8,128)S(1)} %copy.132), channel_id=1, source_target_pairs={{0,1},{1,2},{2,3},{4,5},{5,6},{6,7},{8,9},{9,10},{10,11},{12,13},{... | collective-permute-start | bytes 32648 | tf_op jit(solution)/shard_map/ppermute | solution.py:14
  116.6 7.4 %collective-permute-start.6 = (f32[8,1,32,128]{3,0,2,1:T(8,128)S(1)}, f32[8,1,32,128]{3,0,2,1:T(8,128)S(1)}, u32[]{:S(2)}, u32[]{:S(2)}) collective-permute-start(f32[8,1,32,128]{3,0,2,1:T(8,128)S(1)} %get-tuple-element.83), channel_id=1, source_target_pairs={{8,0},{16,8},{24,16},{9,1},{17,9},{25,17},{10,2},{18,10},{26,18},{... | collective-permute-start | bytes 393224 | tf_op jit(solution)/shard_map/ppermute | solution.py:17
  117.9 7.3 %collective-permute-start.7 = (f32[8,1,32,128]{3,0,2,1:T(8,128)S(1)}, f32[8,1,32,128]{3,0,2,1:T(8,128)S(1)}, u32[]{:S(2)}, u32[]{:S(2)}) collective-permute-start(f32[8,1,32,128]{3,0,2,1:T(8,128)S(1)} %get-tuple-element.82), channel_id=1, source_target_pairs={{0,8},{8,16},{16,24},{1,9},{9,17},{17,25},{2,10},{10,18},{18,26},{... | collective-permute-start | bytes 393224 | tf_op jit(solution)/shard_map/ppermute | solution.py:14
  124.0 6.4 %copy-start.1 = (f32[8,1,32,128]{3,0,2,1:T(8,128)}, f32[8,1,32,128]{3,0,2,1:T(8,128)S(1)}, u32[]{:S(2)}) copy-start(f32[8,1,32,128]{3,0,2,1:T(8,128)S(1)} %collective-permute-done.6) | copy-start | bytes 393220
  125.2 5.2 %copy-start.2 = (f32[8,1,32,128]{3,0,2,1:T(8,128)}, f32[8,1,32,128]{3,0,2,1:T(8,128)S(1)}, u32[]{:S(2)}) copy-start(f32[8,1,32,128]{3,0,2,1:T(8,128)S(1)} %collective-permute-done.7) | copy-start | bytes 393220
  125.2 4.4 %collective-permute-start.8 = (f32[8,10,1,128]{3,0,2,1:T(8,128)S(1)}, f32[8,10,1,128]{3,0,2,1:T(8,128)S(1)}, u32[]{:S(2)}, u32[]{:S(2)}) collective-permute-start(f32[8,10,1,128]{3,0,2,1:T(8,128)S(1)} %get-tuple-element.79), channel_id=1, source_target_pairs={{4,0},{5,1},{6,2},{7,3},{12,8},{13,9},{14,10},{15,11},{20,16},{21,... | collective-permute-start | bytes 122888 | tf_op jit(solution)/shard_map/ppermute | solution.py:17
  126.5 3.9 %collective-permute-start.9 = (f32[8,10,1,128]{3,0,2,1:T(8,128)S(1)}, f32[8,10,1,128]{3,0,2,1:T(8,128)S(1)}, u32[]{:S(2)}, u32[]{:S(2)}) collective-permute-start(f32[8,10,1,128]{3,0,2,1:T(8,128)S(1)} %get-tuple-element.78), channel_id=1, source_target_pairs={{0,4},{1,5},{2,6},{3,7},{8,12},{9,13},{10,14},{11,15},{16,20},{17,... | collective-permute-start | bytes 122888 | tf_op jit(solution)/shard_map/ppermute | solution.py:14
  130.4 0.6 copy-start.5
  135.3 9.4 %collective-permute-start.10 = (f32[8,10,34,1]{2,0,3,1:T(8,128)}, f32[8,10,34,1]{2,0,3,1:T(8,128)}, u32[]{:S(2)}, u32[]{:S(2)}) collective-permute-start(f32[8,10,34,1]{2,0,3,1:T(8,128)} %copy.137), channel_id=1, source_target_pairs={{1,0},{2,1},{3,2},{5,4},{6,5},{7,6},{9,8},{10,9},{11,10},{13,12},{... | collective-permute-start | bytes 32648 | tf_op jit(solution)/shard_map/ppermute | solution.py:17
  137.8 8.3 %collective-permute-start.11 = (f32[8,10,34,1]{2,0,3,1:T(8,128)}, f32[8,10,34,1]{2,0,3,1:T(8,128)}, u32[]{:S(2)}, u32[]{:S(2)}) collective-permute-start(f32[8,10,34,1]{2,0,3,1:T(8,128)} %copy.139), channel_id=1, source_target_pairs={{0,1},{1,2},{2,3},{4,5},{5,6},{6,7},{8,9},{9,10},{10,11},{12,13},{... | collective-permute-start | bytes 32648 | tf_op jit(solution)/shard_map/ppermute | solution.py:14
